TPU v7x, 32 devices: a whole 2x2x4 slice. The times are simulated.
32 devices in a mesh: groups: 2 (over x), rows: 16 (over z, y, core).
Axes of the slice: x: 2, y: 2, z: 4, core: 2. Of those that a mesh axis runs over, the one named last changes fastest.
Arguments:
- phase: float32 [512, 2048], P(('groups', 'rows')), parts along dimension 0, may hold values from -3.140625 to 3.140625
Outputs:
- filtered: float32 [2, 512, 2048], P(None, ('groups', 'rows')), parts along dimension 1
- profile: float32 [6, 16], P('groups'), parts along dimension 0
There are 2 independent parts, one for each index of `groups`. A program takes and returns all parts, laid end to end along the dimension named above; each array names one. Nothing has to cross between parts.
All inputs are finite; a program needn't handle non-finite values.
Results may differ from a plain program's by a relative error of at most 0.00012.
Values sent between devices are 32-bit elements; how exact they have to be, the bound alone decides.
A program may use at most 64 MiB of HBM per device.

v0:
```python
import functools
import math

import jax
import jax.numpy as jnp
from jax import lax
from jax.experimental import pallas as pl
from jax.experimental.pallas import tpu as pltpu
from jax.sharding import PartitionSpec as P

ITERS = 3
HALF = 16
WIN = 32
EPS = 1e-06
REACH = ITERS
SLABS = 2 * REACH + 1


def rotated(value, cosine, sine):
    real, imag = value
    if sine == 0.0:
        return value
    if cosine == 0.0:
        return (imag, -real) if sine > 0 else (-imag, real)
    if abs(cosine - sine) < 1e-12:
        return ((real + imag) * cosine, (imag - real) * cosine)
    if abs(cosine + sine) < 1e-12:
        return ((real - imag) * cosine, (imag + real) * cosine)
    return (real * cosine + imag * sine, imag * cosine - real * sine)


def twiddle(power, size):
    power = power % size
    exact = {0: (1.0, 0.0), size // 4: (0.0, 1.0), size // 2: (-1.0, 0.0), 3 * size // 4: (0.0, -1.0)}
    if power in exact:
        return exact[power]
    angle = 2.0 * math.pi * power / size
    return math.cos(angle), math.sin(angle)


def plus(a, b):
    return (a[0] + b[0], a[1] + b[1])


def minus(a, b):
    return (a[0] - b[0], a[1] - b[1])


def fft(values):
    size = len(values)
    if size == 1:
        return values
    if size == 2:
        return [plus(values[0], values[1]), minus(values[0], values[1])]
    even = fft(values[0::2])
    first = fft(values[1::4])
    third = fft(values[3::4])
    quarter = size // 4
    result = [None] * size
    for k in range(quarter):
        p = rotated(first[k], *twiddle(k, size))
        q = rotated(third[k], *twiddle(3 * k, size))
        total = plus(p, q)
        gap = minus(p, q)
        result[k] = plus(even[k], total)
        result[k + 2 * quarter] = minus(even[k], total)
        base = even[k + quarter]
        result[k + quarter] = (base[0] + gap[1], base[1] - gap[0])
        result[k + 3 * quarter] = (base[0] - gap[1], base[1] + gap[0])
    return result


def inverse_fft(values):
    swapped = fft([(imag, real) for real, imag in values])
    return [(real, imag) for imag, real in swapped]


def ramp(offset):
    return 1.0 - abs(offset - (WIN - 1) / 2) / HALF


SIN = [(-1.0) ** k / math.factorial(2 * k + 1) for k in range(7)]
COS = [(-1.0) ** k / math.factorial(2 * k) for k in range(8)]


def polynomial(coefficients, x):
    total = coefficients[-1]
    for c in coefficients[-2::-1]:
        total = total * x + c
    return total


def cos_sin(x):
    u = x * 0.5
    u2 = u * u
    s = u * polynomial(SIN, u2)
    c = polynomial(COS, u2)
    return 1.0 - 2.0 * s * s, 2.0 * s * c


def kernel(n, lanes, ph_ref, out_ref, prof_ref, ph, z, spec, cols, mine, heard,
           send_sem, recv_sem, tell_sem, hear_sem):
    me = lax.axis_index("rows")

    def inside(index):
        return jnp.logical_and(index >= 0, index < n)

    barrier = pltpu.get_barrier_semaphore()

    @pl.loop(1, n)
    def _(d):
        other = lax.rem(me + d, n)
        pl.semaphore_signal(barrier, inc=1, device_id={"rows": other}, device_id_type=pl.DeviceIdType.MESH)

    lane = lax.broadcasted_iota(jnp.int32, (8, lanes), 1)

    def next_block(x):
        return jnp.where(lane == lanes - 1, 0.0, pltpu.roll(x, lanes - 1, 1))

    def last_block(x):
        return jnp.where(lane == 0, 0.0, pltpu.roll(x, 1, 1))

    def enter(source, slot):
        @pl.loop(0, HALF)
        def _(t):
            for h in range(2):
                x = source[pl.ds(t * HALF + 8 * h, 8), :]
                c, s = cos_sin(x)
                z[0, slot, 0, pl.ds(t * HALF + 8 * h, 8), :] = c
                z[0, slot, 1, pl.ds(t * HALF + 8 * h, 8), :] = s

    def clear(buffer, slot):
        z[buffer, slot] = jnp.zeros((2, HALF * HALF, lanes), jnp.float32)

    enter(ph_ref, REACH)
    for slot in range(1, SLABS - 1):
        clear(1, slot)
    pl.semaphore_wait(barrier, n - 1)

    def copy(d):
        return pltpu.make_async_remote_copy(
            src_ref=ph_ref,
            dst_ref=ph.at[REACH - d],
            send_sem=send_sem.at[REACH - d],
            recv_sem=recv_sem.at[REACH - d],
            device_id={"rows": me + d},
            device_id_type=pl.DeviceIdType.MESH,
        )

    order = [d for k in range(1, REACH + 1) for d in (-k, k)]
    for d in order:
        @pl.when(inside(me + d))
        def _(d=d):
            copy(d).start()

    def arrive(d):
        slot = REACH + d
        valid = inside(me + d)

        @pl.when(valid)
        def _():
            pltpu.make_async_remote_copy(
                src_ref=ph_ref,
                dst_ref=ph.at[slot],
                send_sem=send_sem.at[slot],
                recv_sem=recv_sem.at[slot],
                device_id={"rows": me + d},
                device_id_type=pl.DeviceIdType.MESH,
            ).wait_recv()
            enter(ph.at[slot], slot)

        @pl.when(jnp.logical_not(valid))
        def _():
            clear(0, slot)

    def profile(buffer, step):
        def row(slot, t):
            real = z[buffer, slot, 0, pl.ds(t * HALF, HALF), :]
            imag = z[buffer, slot, 1, pl.ds(t * HALF, HALF), :]

            def after(x):
                first = next_block(x[0:8])[0:1]
                return jnp.concatenate([x[1:], first], axis=0)

            return real, imag, after(real), after(imag)

        def cross(ar, ai, br, bi):
            return ai * br - ar * bi

        def add(upper, lower, total):
            loop = (
                cross(upper[0], upper[1], upper[2], upper[3])
                + cross(upper[2], upper[3], lower[2], lower[3])
                + cross(lower[2], lower[3], lower[0], lower[1])
                + cross(lower[0], lower[1], upper[0], upper[1])
            )
            return total + loop * loop

        total = lax.fori_loop(
            0, HALF - 1,
            lambda t, total: add(row(REACH, t), row(REACH, t + 1), total),
            jnp.zeros((HALF, lanes), jnp.float32),
        )
        total = add(row(REACH, HALF - 1), row(REACH + 1, 0), total)
        mine[pl.ds(step, 1), :] = jnp.sum(total, axis=0, keepdims=True)

    def window_row(buffer, w):
        upper = REACH + w

        energy = jnp.zeros((8, lanes), jnp.float32)
        for h in range(2):
            values = []
            for t in range(WIN):
                at = pl.ds((t % HALF) * HALF + 8 * h, 8)
                values.append((z[buffer, upper + t // HALF, 0, at, :], z[buffer, upper + t // HALF, 1, at, :]))
            for real, imag in values:
                energy = energy + (real * real + imag * imag)
            for k, value in enumerate(fft(values)):
                for c in range(2):
                    spec[c, pl.ds(k * WIN + 8 * h, 8), :] = value[c]
                    spec[c, pl.ds(k * WIN + HALF + 8 * h, 8), :] = next_block(value[c])
        energy = jnp.broadcast_to(jnp.sum(energy, axis=0, keepdims=True), (8, lanes))
        scale = 1.0 / (energy + next_block(energy) + EPS)

        @pl.loop(0, WIN // 8)
        def _(g):
            values = []
            for s in range(WIN):
                at = pl.ds(g * 8 * WIN + s, 8, stride=WIN)
                values.append((spec[0, at, :], spec[1, at, :]))
            shaped = []
            for real, imag in fft(values):
                ratio = jnp.maximum((real * real + imag * imag) * scale, 1e-37)
                gain = lax.rsqrt(lax.rsqrt(ratio))
                shaped.append((real * gain, imag * gain))
            back = inverse_fft(shaped)
            for s in range(HALF):
                near = ramp(s) / (WIN * WIN)
                far = ramp(s + HALF) / (WIN * WIN)
                for c in range(2):
                    joined = back[s][c] * near + last_block(back[s + HALF][c] * far)
                    cols[c, pl.ds(g * 8 * HALF + s, 8, stride=HALF), :] = joined

        for h in range(2):
            values = []
            for k in range(WIN):
                at = pl.ds(k * HALF + 8 * h, 8)
                values.append((cols[0, at, :], cols[1, at, :]))
            for t, value in enumerate(inverse_fft(values)):
                at = pl.ds((t % HALF) * HALF + 8 * h, 8)
                for c in range(2):
                    z[1 - buffer, upper + t // HALF, c, at, :] += value[c] * ramp(t)

        @pl.when(me + w + 1 == n)
        def _():
            clear(1 - buffer, upper + 1)

    mine[...] = jnp.zeros_like(mine)
    arrive(1)
    profile(0, 0)

    @pl.loop(0, 2 * REACH)
    def _(k):
        half = k // 2
        odd = lax.rem(k, 2)

        @pl.when(k > 0)
        def _():
            arrive(jnp.where(odd == 1, -half - 1, half + 1))

        w = jnp.where(odd == 1, -half - 1, half)

        @pl.when(inside(me + w))
        def _():
            window_row(0, w)

    def tell(d):
        other = lax.rem(me + d, n)
        return pltpu.make_async_remote_copy(
            src_ref=mine,
            dst_ref=heard.at[n - d],
            send_sem=tell_sem.at[d],
            recv_sem=hear_sem.at[n - d],
            device_id={"rows": other},
            device_id_type=pl.DeviceIdType.MESH,
        )

    for step in range(1, ITERS):
        buffer = step % 2
        reach = REACH - step
        profile(buffer, step)
        for slot in range(REACH - reach, REACH + reach + 1):
            clear(1 - buffer, slot)

        @pl.loop(-reach, reach)
        def _(w):
            @pl.when(inside(me + w))
            def _():
                window_row(buffer, w)

            if step == ITERS - 1:
                @pl.when(w == -reach)
                def _():
                    @pl.loop(1, n)
                    def _(d):
                        tell(d).start()

    out_ref[...] = z[ITERS % 2, REACH]

    for d in order:
        @pl.when(inside(me + d))
        def _(d=d):
            copy(d).wait_send()

    def listen(d, total):
        tell(d).wait_send()
        pltpu.make_async_remote_copy(
            src_ref=mine,
            dst_ref=heard.at[d],
            send_sem=tell_sem.at[d],
            recv_sem=hear_sem.at[d],
            device_id={"rows": lax.rem(me + d, n)},
            device_id_type=pl.DeviceIdType.MESH,
        ).wait_recv()
        return total + heard[d]

    prof_ref[...] = lax.fori_loop(1, n, listen, mine[...])


def per_device(n, phase):
    slab, width = phase.shape
    assert slab == HALF
    lanes = width // HALF
    turned = phase.reshape(slab, lanes, HALF).transpose(0, 2, 1).reshape(slab * HALF, lanes)
    area = HALF * HALF
    field, sums = pl.pallas_call(
        functools.partial(kernel, n, lanes),
        out_shape=(
            jax.ShapeDtypeStruct((2, area, lanes), jnp.float32),
            jax.ShapeDtypeStruct((8, lanes), jnp.float32),
        ),
        in_specs=[pl.BlockSpec(memory_space=pltpu.VMEM)],
        out_specs=(pl.BlockSpec(memory_space=pltpu.VMEM), pl.BlockSpec(memory_space=pltpu.VMEM)),
        scratch_shapes=[
            pltpu.VMEM((SLABS, area, lanes), jnp.float32),
            pltpu.VMEM((2, SLABS, 2, area, lanes), jnp.float32),
            pltpu.VMEM((2, WIN * WIN, lanes), jnp.float32),
            pltpu.VMEM((2, WIN * HALF, lanes), jnp.float32),
            pltpu.VMEM((8, lanes), jnp.float32),
            pltpu.VMEM((n, 8, lanes), jnp.float32),
            pltpu.SemaphoreType.DMA((SLABS,)),
            pltpu.SemaphoreType.DMA((SLABS,)),
            pltpu.SemaphoreType.DMA((n,)),
            pltpu.SemaphoreType.DMA((n,)),
        ],
        compiler_params=pltpu.CompilerParams(collective_id=0, has_side_effects=True),
    )(turned)
    filtered = field.reshape(2, slab, HALF, lanes).transpose(0, 1, 3, 2).reshape(2, slab, width)
    per_tile = 128 // HALF
    tiles = sums[:ITERS].reshape(ITERS, lanes // per_tile, per_tile).sum(axis=2)
    return filtered, tiles / (slab * n * 128.0)


def solution(mesh):
    return jax.shard_map(
        functools.partial(per_device, mesh.shape["rows"]),
        mesh=mesh,
        in_specs=(P(("groups", "rows"), None),),
        out_specs=(P(None, ("groups", "rows"), None), P("groups", None)),
        check_vma=False,
    )
```

profile of v0, /device:TPU:0, one launch (start us, length us, event | category | flops | bytes accessed | tf_op | source)
XLA Modules:
  0.0 56.5 jit_solution(11409324817530299322)
XLA Ops:
  0.6 1.3 %reshape.19 = f32[16,128,16]{2,1,0:T(8,128)S(1)} reshape(f32[16,2048]{1,0:T(8,128)} %param.1) | data formatting | bytes 262144 | tf_op jit(solution)/shard_map/reshape | solution.py:334
  1.9 1.0 %copy.5 = f32[16,16,128]{2,1,0:T(8,128)} copy(f32[16,16,128]{1,2,0:T(8,128)S(1)} %bitcast.7) | data formatting | bytes 262144 | tf_op jit(solution)/shard_map/transpose | solution.py:334
  2.9 48.4 %shard_map.30 = (f32[2,256,128]{2,1,0:T(8,128)}, f32[8,128]{1,0:T(8,128)}) custom-call(f32[256,128]{1,0:T(8,128)} %bitcast.8), custom_call_target="tpu_custom_call" | custom-call | tf_op jit(solution)/shard_map/pallas_call | solution.py:336
  51.2 0.7 %slice.3 = f32[3,128]{1,0:T(4,128)S(1)} slice(f32[8,128]{1,0:T(8,128)} %get-tuple-element.5), slice={[0:3], [0:128]} | slice | bytes 3072 | tf_op jit(solution)/shard_map/slice | solution.py:360
  51.9 0.1 reshape.23
  52.0 0.1 reduce_sum.9
  52.1 0.6 %broadcast_multiply_fusion = f32[3,16]{1,0:T(4,128)} fusion(f32[3,16]{1,0:T(4,128)S(1)} %reduce_sum.9), kind=kLoop, calls=%fused_computation | loop fusion | flops 48 | bytes 384 | tf_op jit(solution)/shard_map/div | solution.py:361
  52.7 1.5 %copy.6 = f32[2,16,16,128]{2,3,1,0:T(8,128)S(1)} copy(f32[2,16,16,128]{3,2,1,0:T(8,128)} %bitcast.9) | data formatting | bytes 524288 | tf_op jit(solution)/shard_map/reshape | solution.py:358
  54.2 2.3 %reshape.22 = f32[2,16,2048]{2,1,0:T(8,128)} reshape(f32[2,16,128,16]{3,2,1,0:T(8,128)S(1)} %bitcast.6) | data formatting | bytes 524288 | tf_op jit(solution)/shard_map/reshape | solution.py:358
where the time goes:
time: 56.7 us; the launch traced here: 56.5 us
  Pallas kernels  48.4 us (85%)
  local copies, waits for them, and re-layouts  6.8 us (12%)
  other arithmetic  0.68 us (1%)
  between operations  0.66 us (1%)
    pallas_call x1, Pallas kernels, per_device(): pl.pallas_call(functools.partial(kernel, n, lanes), out_shape=(jax.ShapeD...  48.4 us
    reshape x2, local copies, waits for them, and re-layouts, per_device(): field.reshape(2, slab, HALF, lanes).transpose(0, 1, 3, 2)  3.81 us
    reshape x1, local copies, waits for them, and re-layouts, per_device(): phase.reshape(slab, lanes, HALF).transpose(0, 2, 1)  1.26 us

commit v1 on v0

--- a/solution.py
+++ b/solution.py
@@ -14,6 +14,7 @@
 EPS = 1e-06
 REACH = ITERS
 SLABS = 2 * REACH + 1
+PITCH = HALF + 1
 
 
 def rotated(value, cosine, sine):
@@ -217,17 +218,17 @@
                 energy = energy + (real * real + imag * imag)
             for k, value in enumerate(fft(values)):
                 for c in range(2):
-                    spec[c, pl.ds(k * WIN + 8 * h, 8), :] = value[c]
-                    spec[c, pl.ds(k * WIN + HALF + 8 * h, 8), :] = next_block(value[c])
+                    spec[c, pl.ds(k * PITCH + 8 * h, 8), :] = value[c]
         energy = jnp.broadcast_to(jnp.sum(energy, axis=0, keepdims=True), (8, lanes))
         scale = 1.0 / (energy + next_block(energy) + EPS)
 
         @pl.loop(0, WIN // 8)
         def _(g):
             values = []
-            for s in range(WIN):
-                at = pl.ds(g * 8 * WIN + s, 8, stride=WIN)
+            for s in range(HALF):
+                at = pl.ds(g * 8 * PITCH + s, 8, stride=PITCH)
                 values.append((spec[0, at, :], spec[1, at, :]))
+            values += [(next_block(real), next_block(imag)) for real, imag in values]
             shaped = []
             for real, imag in fft(values):
                 ratio = jnp.maximum((real * real + imag * imag) * scale, 1e-37)
@@ -239,12 +240,12 @@
                 far = ramp(s + HALF) / (WIN * WIN)
                 for c in range(2):
                     joined = back[s][c] * near + last_block(back[s + HALF][c] * far)
-                    cols[c, pl.ds(g * 8 * HALF + s, 8, stride=HALF), :] = joined
+                    cols[c, pl.ds(g * 8 * PITCH + s, 8, stride=PITCH), :] = joined
 
         for h in range(2):
             values = []
             for k in range(WIN):
-                at = pl.ds(k * HALF + 8 * h, 8)
+                at = pl.ds(k * PITCH + 8 * h, 8)
                 values.append((cols[0, at, :], cols[1, at, :]))
             for t, value in enumerate(inverse_fft(values)):
                 at = pl.ds((t % HALF) * HALF + 8 * h, 8)
@@ -324,7 +325,14 @@
         ).wait_recv()
         return total + heard[d]
 
-    prof_ref[...] = lax.fori_loop(1, n, listen, mine[...])
+    sums = lax.fori_loop(1, n, listen, mine[...])
+    tiles = prof_ref.shape[1]
+    per_tile = lanes // tiles
+    rows = lax.broadcasted_iota(jnp.int32, (lanes, tiles), 0)
+    low = lax.broadcasted_iota(jnp.int32, (lanes, tiles), 1) * per_tile
+    member = jnp.where(jnp.logical_and(rows >= low, rows < low + per_tile), 1.0, 0.0)
+    energy = jnp.dot(sums, member, precision=lax.Precision.HIGHEST, preferred_element_type=jnp.float32)
+    prof_ref[...] = energy[:ITERS] / (HALF * n * 128.0)
 
 
 def per_device(n, phase):
@@ -333,19 +341,19 @@
     lanes = width // HALF
     turned = phase.reshape(slab, lanes, HALF).transpose(0, 2, 1).reshape(slab * HALF, lanes)
     area = HALF * HALF
-    field, sums = pl.pallas_call(
+    field, profile = pl.pallas_call(
         functools.partial(kernel, n, lanes),
         out_shape=(
             jax.ShapeDtypeStruct((2, area, lanes), jnp.float32),
-            jax.ShapeDtypeStruct((8, lanes), jnp.float32),
+            jax.ShapeDtypeStruct((ITERS, width // 128), jnp.float32),
         ),
         in_specs=[pl.BlockSpec(memory_space=pltpu.VMEM)],
         out_specs=(pl.BlockSpec(memory_space=pltpu.VMEM), pl.BlockSpec(memory_space=pltpu.VMEM)),
         scratch_shapes=[
             pltpu.VMEM((SLABS, area, lanes), jnp.float32),
             pltpu.VMEM((2, SLABS, 2, area, lanes), jnp.float32),
-            pltpu.VMEM((2, WIN * WIN, lanes), jnp.float32),
-            pltpu.VMEM((2, WIN * HALF, lanes), jnp.float32),
+            pltpu.VMEM((2, WIN * PITCH, lanes), jnp.float32),
+            pltpu.VMEM((2, WIN * PITCH, lanes), jnp.float32),
             pltpu.VMEM((8, lanes), jnp.float32),
             pltpu.VMEM((n, 8, lanes), jnp.float32),
             pltpu.SemaphoreType.DMA((SLABS,)),
@@ -356,9 +364,7 @@
         compiler_params=pltpu.CompilerParams(collective_id=0, has_side_effects=True),
     )(turned)
     filtered = field.reshape(2, slab, HALF, lanes).transpose(0, 1, 3, 2).reshape(2, slab, width)
-    per_tile = 128 // HALF
-    tiles = sums[:ITERS].reshape(ITERS, lanes // per_tile, per_tile).sum(axis=2)
-    return filtered, tiles / (slab * n * 128.0)
+    return filtered, profile
 
 
 def solution(mesh):

time: 56.7 us -> 52.7 us (0.929)
  Pallas kernels: 48.4 us -> 45.3 us
  other arithmetic: 0.68 us -> 0 us
    pallas_call x1, Pallas kernels: 48.4 us -> 45.3 us  [per_device(): pl.pallas_call(functools.partial(kernel, n, lanes), out_shape=(jax.ShapeD...]
    slice x1 -> x0, local copies, waits for them, and re-layouts: 0.68 us -> none  [per_device(): tiles = sums[:ITERS].reshape(ITERS, lanes // per_tile, per_tile).sum(axis=2)]
    div x1 -> x0, other arithmetic: 0.59 us -> none  [per_device(): return (filtered, tiles / (slab * n * 128.0))]
    unnamed x0 -> x3, local copies, waits for them, and re-layouts: none -> 0.58 us
where the time goes in v1:
time: 52.7 us; the launch traced here: 52.6 us
  Pallas kernels  45.3 us (86%)
  local copies, waits for them, and re-layouts  6.62 us (13%)
  between operations  0.66 us (1%)
    pallas_call x1, Pallas kernels, per_device(): pl.pallas_call(functools.partial(kernel, n, lanes), out_shape=(jax.ShapeD...  45.3 us
    reshape x2, local copies, waits for them, and re-layouts, per_device(): field.reshape(2, slab, HALF, lanes).transpose(0, 1, 3, 2)  3.81 us
    reshape x1, local copies, waits for them, and re-layouts, per_device(): phase.reshape(slab, lanes, HALF).transpose(0, 2, 1)  1.26 us

profile of v1, /device:TPU:0, one launch (start us, length us, event | category | flops | bytes accessed | tf_op | source)
XLA Modules:
  0.0 52.6 jit_solution(3021615099699783049)
XLA Ops:
  0.6 1.3 %reshape.16 = f32[16,128,16]{2,1,0:T(8,128)S(1)} reshape(f32[16,2048]{1,0:T(8,128)} %param.1) | data formatting | bytes 262144 | tf_op jit(solution)/shard_map/reshape | solution.py:342
  1.9 1.0 %copy.5 = f32[16,16,128]{2,1,0:T(8,128)} copy(f32[16,16,128]{1,2,0:T(8,128)S(1)} %bitcast.7) | data formatting | bytes 262144 | tf_op jit(solution)/shard_map/transpose | solution.py:342
  2.9 45.3 %shard_map.30 = (f32[2,256,128]{2,1,0:T(8,128)}, f32[3,16]{1,0:T(4,128)}) custom-call(f32[256,128]{1,0:T(8,128)} %bitcast.8), custom_call_target="tpu_custom_call" | custom-call | tf_op jit(solution)/shard_map/pallas_call | solution.py:344
  48.2 0.0 copy-start
  48.2 1.5 %copy.6 = f32[2,16,16,128]{2,3,1,0:T(8,128)S(1)} copy(f32[2,16,16,128]{3,2,1,0:T(8,128)} %bitcast.9) | data formatting | bytes 524288 | tf_op jit(solution)/shard_map/reshape | solution.py:366
  49.7 2.3 %reshape.19 = f32[2,16,2048]{2,1,0:T(8,128)} reshape(f32[2,16,128,16]{3,2,1,0:T(8,128)S(1)} %bitcast.6) | data formatting | bytes 524288 | tf_op jit(solution)/shard_map/reshape | solution.py:366
  52.0 0.0 copy-done
  52.0 0.6 %copy.8 = f32[3,16]{1,0:T(4,128)} copy(f32[3,16]{1,0:T(4,128)S(1)} %copy-done) | data formatting | bytes 384
Async XLA Ops:
  48.2 3.8 %copy-start = (f32[3,16]{1,0:T(4,128)S(1)}, f32[3,16]{1,0:T(4,128)}, u32[]{:S(2)}) copy-start(f32[3,16]{1,0:T(4,128)} %get-tuple-element.9) | copy-start | bytes 580

commit v2 on v1

--- a/solution.py
+++ b/solution.py
@@ -15,6 +15,8 @@
 REACH = ITERS
 SLABS = 2 * REACH + 1
 PITCH = HALF + 1
+AREA = HALF * HALF
+SKEW = 8
 
 
 def rotated(value, cosine, sine):
@@ -131,43 +133,61 @@
                 z[0, slot, 1, pl.ds(t * HALF + 8 * h, 8), :] = s
 
     def clear(buffer, slot):
-        z[buffer, slot] = jnp.zeros((2, HALF * HALF, lanes), jnp.float32)
+        for c in range(2):
+            z[buffer, slot, c, 0:AREA] = jnp.zeros((AREA, lanes), jnp.float32)
 
     enter(ph_ref, REACH)
     for slot in range(1, SLABS - 1):
         clear(1, slot)
     pl.semaphore_wait(barrier, n - 1)
 
-    def copy(d):
+    side = 1 - 2 * lax.rem(me, 2)
+
+    def copy(source, d, target, index):
+        slot = REACH + d - target
+        return pltpu.make_async_remote_copy(
+            src_ref=source,
+            dst_ref=ph.at[slot],
+            send_sem=send_sem.at[index],
+            recv_sem=recv_sem.at[slot],
+            device_id={"rows": me + target},
+            device_id_type=pl.DeviceIdType.MESH,
+        )
+
+    direct = [(side, 0), (2 * side, 1), (-2 * side, 2), (-3 * side, 3)]
+    relayed = [(2 * side, 4), (-2 * side, 5)]
+
+    for target, index in direct:
+        @pl.when(inside(me + target))
+        def _(target=target, index=index):
+            copy(ph_ref, 0, target, index).start()
+
+    def landed(d):
+        slot = REACH + d
         return pltpu.make_async_remote_copy(
             src_ref=ph_ref,
-            dst_ref=ph.at[REACH - d],
-            send_sem=send_sem.at[REACH - d],
-            recv_sem=recv_sem.at[REACH - d],
+            dst_ref=ph.at[slot],
+            send_sem=send_sem.at[0],
+            recv_sem=recv_sem.at[slot],
             device_id={"rows": me + d},
             device_id_type=pl.DeviceIdType.MESH,
         )
 
-    order = [d for k in range(1, REACH + 1) for d in (-k, k)]
-    for d in order:
-        @pl.when(inside(me + d))
-        def _(d=d):
-            copy(d).start()
-
-    def arrive(d):
+    def relay():
+        for d, index in relayed:
+            @pl.when(inside(me + d))
+            def _(d=d, index=index):
+                landed(d).wait_recv()
+                copy(ph.at[REACH + d], d, side, index).start()
+
+    def arrive(d, waited):
         slot = REACH + d
         valid = inside(me + d)
 
         @pl.when(valid)
         def _():
-            pltpu.make_async_remote_copy(
-                src_ref=ph_ref,
-                dst_ref=ph.at[slot],
-                send_sem=send_sem.at[slot],
-                recv_sem=recv_sem.at[slot],
-                device_id={"rows": me + d},
-                device_id_type=pl.DeviceIdType.MESH,
-            ).wait_recv()
+            if not waited:
+                landed(d).wait_recv()
             enter(ph.at[slot], slot)
 
         @pl.when(jnp.logical_not(valid))
@@ -257,23 +277,49 @@
             clear(1 - buffer, upper + 1)
 
     mine[...] = jnp.zeros_like(mine)
-    arrive(1)
+
+    def first_pass(slab, window, waited):
+        arrive(slab * side, waited)
+        w = window * side + (side - 1) // 2
+
+        @pl.when(inside(me + w))
+        def _():
+            window_row(0, w)
+
+    first_pass(1, 0, False)
+    relay()
+    first_pass(2, 1, True)
+
+    @pl.loop(0, 2)
+    def _(k):
+        w = -1 - k
+        slab = (-1 - k) * side
+
+        @pl.when(k == 0)
+        def _():
+            arrive(slab, False)
+
+        @pl.when(k == 1)
+        def _():
+            arrive(slab, True)
+
+        below = w * side + (side - 1) // 2
+
+        @pl.when(inside(me + below))
+        def _():
+            window_row(0, below)
+
+    @pl.loop(0, 2)
+    def _(k):
+        slab = (3 - 6 * k) * side
+        arrive(slab, False)
+        below = (2 - 5 * k) * side + (side - 1) // 2
+
+        @pl.when(inside(me + below))
+        def _():
+            window_row(0, below)
+
     profile(0, 0)
-
-    @pl.loop(0, 2 * REACH)
-    def _(k):
-        half = k // 2
-        odd = lax.rem(k, 2)
-
-        @pl.when(k > 0)
-        def _():
-            arrive(jnp.where(odd == 1, -half - 1, half + 1))
-
-        w = jnp.where(odd == 1, -half - 1, half)
-
-        @pl.when(inside(me + w))
-        def _():
-            window_row(0, w)
 
     def tell(d):
         other = lax.rem(me + d, n)
@@ -306,12 +352,18 @@
                     def _(d):
                         tell(d).start()
 
-    out_ref[...] = z[ITERS % 2, REACH]
-
-    for d in order:
+    for c in range(2):
+        out_ref[c] = z[ITERS % 2, REACH, c, 0:AREA]
+
+    for target, index in direct:
+        @pl.when(inside(me + target))
+        def _(target=target, index=index):
+            copy(ph_ref, 0, target, index).wait_send()
+
+    for d, index in relayed:
         @pl.when(inside(me + d))
-        def _(d=d):
-            copy(d).wait_send()
+        def _(d=d, index=index):
+            copy(ph.at[REACH + d], d, side, index).wait_send()
 
     def listen(d, total):
         tell(d).wait_send()
@@ -337,26 +389,25 @@
 
 def per_device(n, phase):
     slab, width = phase.shape
-    assert slab == HALF
+    assert slab == HALF and n % 2 == 0
     lanes = width // HALF
     turned = phase.reshape(slab, lanes, HALF).transpose(0, 2, 1).reshape(slab * HALF, lanes)
-    area = HALF * HALF
     field, profile = pl.pallas_call(
         functools.partial(kernel, n, lanes),
         out_shape=(
-            jax.ShapeDtypeStruct((2, area, lanes), jnp.float32),
+            jax.ShapeDtypeStruct((2, AREA, lanes), jnp.float32),
             jax.ShapeDtypeStruct((ITERS, width // 128), jnp.float32),
         ),
         in_specs=[pl.BlockSpec(memory_space=pltpu.VMEM)],
         out_specs=(pl.BlockSpec(memory_space=pltpu.VMEM), pl.BlockSpec(memory_space=pltpu.VMEM)),
         scratch_shapes=[
-            pltpu.VMEM((SLABS, area, lanes), jnp.float32),
-            pltpu.VMEM((2, SLABS, 2, area, lanes), jnp.float32),
-            pltpu.VMEM((2, WIN * PITCH, lanes), jnp.float32),
-            pltpu.VMEM((2, WIN * PITCH, lanes), jnp.float32),
+            pltpu.VMEM((SLABS, AREA, lanes), jnp.float32),
+            pltpu.VMEM((2, SLABS, 2, AREA + SKEW, lanes), jnp.float32),
+            pltpu.VMEM((2, WIN * PITCH + SKEW, lanes), jnp.float32),
+            pltpu.VMEM((2, WIN * PITCH + SKEW, lanes), jnp.float32),
             pltpu.VMEM((8, lanes), jnp.float32),
             pltpu.VMEM((n, 8, lanes), jnp.float32),
-            pltpu.SemaphoreType.DMA((SLABS,)),
+            pltpu.SemaphoreType.DMA((6,)),
             pltpu.SemaphoreType.DMA((SLABS,)),
             pltpu.SemaphoreType.DMA((n,)),
             pltpu.SemaphoreType.DMA((n,)),

time: 52.7 us -> 48.9 us (0.928)
  Pallas kernels: 45.3 us -> 41.4 us
    pallas_call x1, Pallas kernels: 45.3 us -> 41.4 us  [per_device(): pl.pallas_call(functools.partial(kernel, n, lanes), out_shape=(jax.ShapeD...]
where the time goes in v2:
time: 48.9 us; the launch traced here: 48.7 us
  Pallas kernels  41.4 us (85%)
  local copies, waits for them, and re-layouts  6.62 us (14%)
  between operations  0.66 us (1%)
    pallas_call x1, Pallas kernels, per_device(): pl.pallas_call(functools.partial(kernel, n, lanes), out_shape=(jax.ShapeD...  41.4 us
    reshape x2, local copies, waits for them, and re-layouts, per_device(): field.reshape(2, slab, HALF, lanes).transpose(0, 1, 3, 2)  3.81 us
    reshape x1, local copies, waits for them, and re-layouts, per_device(): phase.reshape(slab, lanes, HALF).transpose(0, 2, 1)  1.26 us

profile of v2, /device:TPU:0, one launch (start us, length us, event | category | flops | bytes accessed | tf_op | source)
XLA Modules:
  0.0 48.7 jit_solution(7882533783226021215)
XLA Ops:
  0.6 1.3 %reshape.16 = f32[16,128,16]{2,1,0:T(8,128)S(1)} reshape(f32[16,2048]{1,0:T(8,128)} %param.1) | data formatting | bytes 262144 | tf_op jit(solution)/shard_map/reshape | solution.py:394
  1.9 1.0 %copy.5 = f32[16,16,128]{2,1,0:T(8,128)} copy(f32[16,16,128]{1,2,0:T(8,128)S(1)} %bitcast.7) | data formatting | bytes 262144 | tf_op jit(solution)/shard_map/transpose | solution.py:394
  2.9 41.4 %shard_map.30 = (f32[2,256,128]{2,1,0:T(8,128)}, f32[3,16]{1,0:T(4,128)}) custom-call(f32[256,128]{1,0:T(8,128)} %bitcast.8), custom_call_target="tpu_custom_call" | custom-call | tf_op jit(solution)/shard_map/pallas_call | solution.py:395
  44.3 0.0 copy-start
  44.3 1.5 %copy.6 = f32[2,16,16,128]{2,3,1,0:T(8,128)S(1)} copy(f32[2,16,16,128]{3,2,1,0:T(8,128)} %bitcast.9) | data formatting | bytes 524288 | tf_op jit(solution)/shard_map/reshape | solution.py:417
  45.8 2.3 %reshape.19 = f32[2,16,2048]{2,1,0:T(8,128)} reshape(f32[2,16,128,16]{3,2,1,0:T(8,128)S(1)} %bitcast.6) | data formatting | bytes 524288 | tf_op jit(solution)/shard_map/reshape | solution.py:417
  48.1 0.0 copy-done
  48.1 0.6 %copy.8 = f32[3,16]{1,0:T(4,128)} copy(f32[3,16]{1,0:T(4,128)S(1)} %copy-done) | data formatting | bytes 384
Async XLA Ops:
  44.3 3.8 %copy-start = (f32[3,16]{1,0:T(4,128)S(1)}, f32[3,16]{1,0:T(4,128)}, u32[]{:S(2)}) copy-start(f32[3,16]{1,0:T(4,128)} %get-tuple-element.9) | copy-start | bytes 580

commit v3 on v2

--- a/solution.py
+++ b/solution.py
@@ -336,21 +336,21 @@
         buffer = step % 2
         reach = REACH - step
         profile(buffer, step)
-        for slot in range(REACH - reach, REACH + reach + 1):
+
+        @pl.loop(REACH - reach, REACH + reach + 1)
+        def _(slot):
             clear(1 - buffer, slot)
+
+        if step == ITERS - 1:
+            @pl.loop(1, n)
+            def _(d):
+                tell(d).start()
 
         @pl.loop(-reach, reach)
         def _(w):
             @pl.when(inside(me + w))
             def _():
                 window_row(buffer, w)
-
-            if step == ITERS - 1:
-                @pl.when(w == -reach)
-                def _():
-                    @pl.loop(1, n)
-                    def _(d):
-                        tell(d).start()
 
     for c in range(2):
         out_ref[c] = z[ITERS % 2, REACH, c, 0:AREA]

time: 48.9 us -> 47.3 us (0.967)
  Pallas kernels: 41.4 us -> 39.8 us
    pallas_call x1, Pallas kernels: 41.4 us -> 39.8 us  [per_device(): pl.pallas_call(functools.partial(kernel, n, lanes), out_shape=(jax.ShapeD...]
where the time goes in v3:
time: 47.3 us; the launch traced here: 47.1 us
  Pallas kernels  39.8 us (84%)
  local copies, waits for them, and re-layouts  6.62 us (14%)
  between operations  0.66 us (1%)
    pallas_call x1, Pallas kernels, per_device(): pl.pallas_call(functools.partial(kernel, n, lanes), out_shape=(jax.ShapeD...  39.8 us
    reshape x2, local copies, waits for them, and re-layouts, per_device(): field.reshape(2, slab, HALF, lanes).transpose(0, 1, 3, 2)  3.81 us
    reshape x1, local copies, waits for them, and re-layouts, per_device(): phase.reshape(slab, lanes, HALF).transpose(0, 2, 1)  1.26 us
    transpose x1, local copies, waits for them, and re-layouts, per_device(): phase.reshape(slab, lanes, HALF).transpose(0, 2, 1)  0.97 us

profile of v3, /device:TPU:0, one launch (start us, length us, event | category | flops | bytes accessed | tf_op | source)
XLA Modules:
  0.0 47.1 jit_solution(8816876081780372202)
XLA Ops:
  0.6 1.3 %reshape.16 = f32[16,128,16]{2,1,0:T(8,128)S(1)} reshape(f32[16,2048]{1,0:T(8,128)} %param.1) | data formatting | bytes 262144 | tf_op jit(solution)/shard_map/reshape | solution.py:394
  1.9 1.0 %copy.5 = f32[16,16,128]{2,1,0:T(8,128)} copy(f32[16,16,128]{1,2,0:T(8,128)S(1)} %bitcast.7) | data formatting | bytes 262144 | tf_op jit(solution)/shard_map/transpose | solution.py:394
  2.9 39.8 %shard_map.30 = (f32[2,256,128]{2,1,0:T(8,128)}, f32[3,16]{1,0:T(4,128)}) custom-call(f32[256,128]{1,0:T(8,128)} %bitcast.8), custom_call_target="tpu_custom_call" | custom-call | tf_op jit(solution)/shard_map/pallas_call | solution.py:395
  42.7 0.0 copy-start
  42.7 1.5 %copy.6 = f32[2,16,16,128]{2,3,1,0:T(8,128)S(1)} copy(f32[2,16,16,128]{3,2,1,0:T(8,128)} %bitcast.9) | data formatting | bytes 524288 | tf_op jit(solution)/shard_map/reshape | solution.py:417
  44.3 2.3 %reshape.19 = f32[2,16,2048]{2,1,0:T(8,128)} reshape(f32[2,16,128,16]{3,2,1,0:T(8,128)S(1)} %bitcast.6) | data formatting | bytes 524288 | tf_op jit(solution)/shard_map/reshape | solution.py:417
  46.5 0.0 copy-done
  46.5 0.6 %copy.8 = f32[3,16]{1,0:T(4,128)} copy(f32[3,16]{1,0:T(4,128)S(1)} %copy-done) | data formatting | bytes 384
Async XLA Ops:
  42.7 3.8 %copy-start = (f32[3,16]{1,0:T(4,128)S(1)}, f32[3,16]{1,0:T(4,128)}, u32[]{:S(2)}) copy-start(f32[3,16]{1,0:T(4,128)} %get-tuple-element.9) | copy-start | bytes 580
